TPU v7x, 16 devices: a whole 2x2x2 slice. The times are simulated.
16 devices in a mesh: dp: 4 (over z, y), tp: 4 (over x, core).
Axes of the slice: x: 2, y: 2, z: 2, core: 2. Of those that a mesh axis runs over, the one named last changes fastest.
Arguments:
- hidden: bfloat16 [4, 2048, 6144], P('dp', 'tp'), parts along dimension 0
- attn_gain: float32 [6144], replicated
- attn_bias: float32 [6144], replicated
- mlp_gain: float32 [6144], replicated
- mlp_bias: float32 [6144], replicated
- w_qkv: bfloat16 [6144, 64, 288], P(None, 'tp')
- w_out: bfloat16 [6144, 6144], P('tp')
- w_up: bfloat16 [6144, 24576], P(None, 'tp')
- w_down: bfloat16 [24576, 6144], P('tp')
- positions: int32 [2048], replicated
Outputs:
- output: bfloat16 [4, 2048, 6144], P('dp', 'tp'), parts along dimension 0
There are 4 independent parts. A program takes and returns all parts, laid end to end along the dimension named above; an argument that names none is the same for every part.
All inputs are finite; a program needn't handle non-finite values.
Results may differ from a plain program's by a relative error of at most 0.00619968.
Values are sent between devices in bfloat16 or wider.
A program may use at most 1 GiB of HBM per device.

v0:
```python
import jax
import jax.numpy as jnp
from jax import lax
from jax.sharding import PartitionSpec as P


def layer_norm(tok_rows, norm_gain, norm_bias):
    rows32 = tok_rows.astype(jnp.float32)
    row_mean = jnp.mean(rows32, axis=-1, keepdims=True)
    centered = rows32 - row_mean
    row_var = jnp.mean(centered * centered, axis=-1, keepdims=True)
    return (centered * lax.rsqrt(row_var + 1e-5) * norm_gain + norm_bias).astype(jnp.bfloat16)


def rotary_tables(positions, head_dim):
    inv_freq = 10000.0 ** (-2.0 * jnp.arange(head_dim // 2, dtype=jnp.float32) / head_dim)
    angles = positions.astype(jnp.float32)[:, None] * inv_freq[None, :]
    angles = jnp.concatenate([angles, angles], axis=-1)
    return jnp.cos(angles), jnp.sin(angles)


def apply_rotary(head_vals, cos_tab, sin_tab):
    half_dim = head_vals.shape[-1] // 2
    vals32 = head_vals.astype(jnp.float32)
    rotated = jnp.concatenate([-vals32[..., half_dim:], vals32[..., :half_dim]], axis=-1)
    return (vals32 * cos_tab + rotated * sin_tab).astype(jnp.bfloat16)


def attention_branch(normed, w_qkv_part, w_out_part, positions):
    batch_size, seq_len, model_width = normed.shape
    num_groups = w_qkv_part.shape[1]
    slot_cols = w_qkv_part.shape[2]
    group_cols = w_out_part.shape[0] // num_groups
    head_dim = (slot_cols - group_cols) // 2
    group_size = group_cols // head_dim
    qkv_rows = jnp.einsum('bsd,dkc->bskc', normed, w_qkv_part, preferred_element_type=jnp.float32).astype(jnp.bfloat16)
    qkv_rows = qkv_rows.reshape(batch_size, seq_len, num_groups, group_size + 2, head_dim)
    cos_tab, sin_tab = rotary_tables(positions, head_dim)
    query_rot = apply_rotary(qkv_rows[:, :, :, :group_size, :], cos_tab[None, :, None, None, :], sin_tab[None, :, None, None, :])
    key_rot = apply_rotary(qkv_rows[:, :, :, group_size, :], cos_tab[None, :, None, :], sin_tab[None, :, None, :])
    value_seq = qkv_rows[:, :, :, group_size + 1, :]
    block_len = min(seq_len, 256)
    num_blocks = seq_len // block_len
    key_idx = jnp.arange(seq_len)
    score_scale = head_dim ** -0.5

    def one_block(block_idx):
        row_start = block_idx * block_len
        query_blk = lax.dynamic_slice_in_dim(query_rot, row_start, block_len, axis=1)
        scores = jnp.einsum('bqkgh,bskh->bkgqs', query_blk, key_rot, preferred_element_type=jnp.float32) * score_scale
        query_idx = row_start + jnp.arange(block_len)
        allowed = key_idx[None, :] <= query_idx[:, None]
        scores = jnp.where(allowed, scores, -1e30)
        exp_scores = jnp.exp(scores - jnp.max(scores, axis=-1, keepdims=True))
        attn_probs = (exp_scores / jnp.sum(exp_scores, axis=-1, keepdims=True)).astype(jnp.bfloat16)
        context = jnp.einsum('bkgqs,bskh->bqkgh', attn_probs, value_seq, preferred_element_type=jnp.float32)
        return context.astype(jnp.bfloat16).reshape(batch_size, block_len, num_groups * group_cols)

    ctx_blocks = lax.map(one_block, jnp.arange(num_blocks))
    attn_part = jnp.einsum('nbqc,cd->bnqd', ctx_blocks, w_out_part, preferred_element_type=jnp.float32)
    return attn_part.reshape(batch_size, seq_len, model_width)


def solution(mesh):
    def local_layer(hidden_blk, attn_gain, attn_bias, mlp_gain, mlp_bias, w_qkv_part, w_out_part, w_up_part, w_down_part, positions):
        normed_attn = layer_norm(hidden_blk, attn_gain, attn_bias)
        normed_mlp = layer_norm(hidden_blk, mlp_gain, mlp_bias)
        attn_in = lax.all_gather(normed_attn, 'tp', axis=1, tiled=True)
        mlp_in = lax.all_gather(normed_mlp, 'tp', axis=1, tiled=True)
        attn_part = attention_branch(attn_in, w_qkv_part, w_out_part, positions)
        up_pre = jnp.einsum('bsd,df->bsf', mlp_in, w_up_part, preferred_element_type=jnp.float32)
        up_act = jax.nn.gelu(up_pre, approximate=False).astype(jnp.bfloat16)
        mlp_part = jnp.einsum('bsf,fd->bsd', up_act, w_down_part, preferred_element_type=jnp.float32)
        token_sum = lax.psum_scatter(attn_part + mlp_part, 'tp', scatter_dimension=1, tiled=True)
        return (hidden_blk.astype(jnp.float32) + token_sum).astype(jnp.bfloat16)

    return jax.shard_map(local_layer, mesh=mesh, in_specs=(P('dp', 'tp', None), P(), P(), P(), P(), P(None, 'tp', None), P('tp', None), P(None, 'tp'), P('tp', None), P()), out_specs=P('dp', 'tp', None), check_vma=False)
```

profile of v0, /device:TPU:0, one launch (start us, length us, event | category | flops | bytes accessed | tf_op | source)
XLA Modules:
  0.0 1642.7 jit_solution(18340972192524384039)
XLA Ops:
  29.3 152.1 %all-gather.3.cloned.1.call-done = bf16[1,2048,6144]{2,1,0:T(8,128)(2,1)} async-done(((bf16[1,512,6144]{2,1,0:T(8,128)(2,1)}), bf16[1,2048,6144]{2,1,0:T(8,128)(2,1)}) %all-gather.3.cloned.1.call-update) | async-done | bytes 25165840 | tf_op jit(solution)/shard_map/all_gather | solution.py:68
  181.4 143.0 %fusion.71 = bf16[2048,16,288]{0,2,1:T(8,128)(2,1)} fusion(bf16[6144,16,288]{0,2,1:T(8,128)(2,1)} %param.17, bf16[1,2048,6144]{2,1,0:T(8,128)(2,1)} %all-gather.3.cloned.1.call-done), kind=kOutput, calls=%fused_computation.84 | convolution fusion | flops 115973554176 | bytes 100663296 | tf_op jit(solution)/shard_map/bsd,dkc->bskc/dot_general | solution.py:36
  324.4 16.8 %slice_bitcast_fusion = (bf16[1,2048,16,96]{1,3,2,0:T(8,128)(2,1)}, f32[1,2048,16,96]{1,3,2,0:T(8,128)}, f32[1,2048,16,1,96]{1,4,2,3,0:T(8,128)}) fusion(bf16[1,2048,16,3,96]{1,4,3,2,0:T(8,128)(2,1)} %bitcast.116), kind=kLoop, calls=%fused_computation.97 | loop fusion | flops 6291456 | bytes 50331648 | tf_op jit(solution)/shard_map/squeeze | solution.py:41
  381.1 393.7 %while.11 = (s32[]{:T(128)}, bf16[8,1,256,1536]{2,3,1,0:T(8,128)(2,1)}, s32[8]{0:T(128)S(1)}, bf16[1,2048,16,1,96]{1,4,2,3,0:T(8,128)(2,1)}, bf16[1,2048,16,96]{...) while((s32[]{:T(128)}, ...), condition=%wide.region_5.6_spmd.clone, body=%wide.region_2.5_spmd.clone.sunk | while | flops 3322798336 | bytes 137447648 | solution.py:59
  382.6 16.3 fusion.132
  398.8 15.9 fusion.133
  431.8 16.3 fusion.132
  448.1 15.9 fusion.133
  481.0 16.3 fusion.132
  497.3 15.9 fusion.133
  530.2 16.3 fusion.132
  546.5 15.9 fusion.133
  579.4 16.3 fusion.132
  595.7 15.9 fusion.133
  628.6 16.3 fusion.132
  644.9 15.9 fusion.133
  677.8 16.3 fusion.132
  694.1 15.9 fusion.133
  727.0 16.3 fusion.132
  743.3 15.9 fusion.133
  774.7 47.7 %fusion.65 = f32[8,256,6144]{2,1,0:T(8,128)} fusion(bf16[1536,6144]{1,0:T(8,128)(2,1)} %param.18, bf16[8,1,256,1536]{2,3,1,0:T(8,128)(2,1)} %get-tuple-element.42), kind=kOutput, calls=%fused_computation.78 | convolution fusion | flops 38654705664 | bytes 75497472 | tf_op jit(solution)/shard_map/nbqc,cd->bnqd/dot_general | solution.py:60
  822.5 171.6 %fusion.31 = f32[2048,6144]{1,0:T(8,128)} fusion(bf16[6144,6144]{1,0:T(8,128)(2,1)} %param.19, bf16[1,2048,6144]{2,1,0:T(8,128)(2,1)} %all-gather.5.cloned.1.call-done), kind=kOutput, calls=%fused_computation.41 | convolution fusion | flops 154618822656 | bytes 150994944 | tf_op jit(solution)/shard_map/bsd,df->bsf/dot_general | solution.py:71
  994.1 302.6 %fusion.29 = f32[1,2048,6144]{2,1,0:T(8,128)} fusion(bf16[6144,6144]{1,0:T(8,128)(2,1)} %param.20, f32[8,256,6144]{2,1,0:T(8,128)} %fusion.65, f32[2048,6144]{1,0:T(8,128)} %fusion.31), kind=kOutput, calls=%fused_computation.40 | convolution fusion | flops 155449294848 | bytes 226492416 | tf_op jit(solution)/shard_map/bsf,fd->bsd/dot_general | solution.py:73
  1296.8 328.1 %reduce-scatter.2.cloned.1.call-done = f32[1,512,6144]{2,1,0:T(8,128)} async-done(((f32[1,2048,6144]{2,1,0:T(8,128)}), f32[1,512,6144]{2,1,0:T(8,128)}) %reduce-scatter.2.cloned.1.call-update) | async-done | bytes 12582928 | tf_op jit(solution)/shard_map/reduce_scatter | solution.py:74
  (105 shorter events, 205.0 us)
Async XLA Ops:
  6.5 18.9 %copy-start = (s32[2048]{0:T(1024)S(1)}, s32[2048]{0:T(1024)}, u32[]{:S(2)}) copy-start(s32[2048]{0:T(1024)} %param.21) | copy-start | bytes 24580
  6.5 174.8 %all-gather.3.cloned.1.call-start = ((), (), s32[]{:S(2)}) async-start(), calls=%async_computation.1 | async-start | bytes 31457280 | tf_op jit(solution)/shard_map/all_gather | solution.py:68
  24.6 797.8 %all-gather.5.cloned.1.call-start = ((), (), s32[]{:S(2)}) async-start(), calls=%async_computation.2 | async-start | bytes 31457280 | tf_op jit(solution)/shard_map/all_gather | solution.py:69
  25.4 1599.5 %reduce-scatter.2.cloned.1.call-start = ((), (), s32[]{:S(2)}) async-start(), calls=%async_computation.3 | async-start | bytes 62914560 | tf_op jit(solution)/shard_map/reduce_scatter | solution.py:74
  398.8 15.9 slice-start
  398.8 15.9 slice-start.1
  448.0 15.9 slice-start
  448.0 15.9 slice-start.1
  497.3 15.9 slice-start
  497.3 15.9 slice-start.1
  546.5 15.9 slice-start
  546.5 15.9 slice-start.1
  595.7 15.9 slice-start
  595.7 15.9 slice-start.1
  644.9 15.9 slice-start
  644.9 15.9 slice-start.1
  694.1 15.9 slice-start
  694.1 15.9 slice-start.1
  743.3 15.9 slice-start
  743.3 15.9 slice-start.1
Sparse Core Ops, SparseCore 0:
  24.8 156.5 all-gather.2
  182.9 153.7 all-gather.4
  1296.9 327.9 reduce-scatter.1
where the time goes:
time: 1650 us; the launch traced here: 1640 us
  matrix products  911 us (55%)
  waiting for transfers between devices  481 us (29%)
  other arithmetic  220 us (13%)
    reduce_scatter x1, waiting for transfers between devices, local_layer(): lax.psum_scatter(attn_part + mlp_part, 'tp', scatter_dimension=1, tiled=T...  328 us
    dot_general x1, matrix products, local_layer(): jnp.einsum('bsf,fd->bsd', up_act, w_down_part, preferred_element_type=jnp...  303 us
    dot_general x1, matrix products, local_layer(): jnp.einsum('bsd,df->bsf', mlp_in, w_up_part, preferred_element_type=jnp.f...  172 us
    all_gather x1, waiting for transfers between devices, local_layer(): attn_in = lax.all_gather(normed_attn, 'tp', axis=1, tiled=True)  152 us
    dot_general x1, matrix products, attention_branch(): jnp.einsum('bsd,dkc->bskc', normed, w_qkv_part, preferred_element_type=jn...  143 us
    dot_general x8, matrix products, one_block(): jnp.einsum('bqkgh,bskh->bkgqs', query_blk, key_rot, preferred_element_typ...  130 us
    reduce_sum x8, other arithmetic, one_block(): jnp.sum(exp_scores, axis=-1, keepdims=True)  127 us
    dot_general x8, matrix products, one_block(): jnp.einsum('bkgqs,bskh->bqkgh', attn_probs, value_seq, preferred_element_...  116 us
  transfers between devices with their start and end apart: 3, of which 2 were waited for; matrix products, arithmetic and copies ran while one was open for 39% of the time, Pallas kernels for 0%

commit v1 on v0

v1 whole, which is shorter than its diff:
```python
import functools

import jax
import jax.numpy as jnp
from jax import lax
from jax.experimental import pallas as pl
from jax.experimental.pallas import tpu as pltpu
from jax.sharding import PartitionSpec as P

F32 = jnp.float32
BF16 = jnp.bfloat16
VMEM_LIMIT = 67_000_000
LOG2E = 1.4426950408889634


def rotary_tables(positions, half_dim):
    inv_freq = 10000.0 ** (-2.0 * jnp.arange(half_dim, dtype=F32) / (2 * half_dim))
    angles = inv_freq[:, None] * positions.astype(F32)[None, :]
    return jnp.cos(angles), jnp.sin(angles)


def peers():
    tp = lax.axis_index('tp')
    mate = tp + 1 - 2 * lax.rem(tp, 2)
    cross = lax.rem(tp + 2, 4)
    return mate, cross


def entry_barrier(mate, cross):
    sem = pltpu.get_barrier_semaphore()
    for dev in (mate, cross):
        pl.semaphore_signal(sem, inc=1, device_id={'tp': dev}, device_id_type=pl.DeviceIdType.MESH)
    pl.semaphore_wait(sem, 2)


def gelu(pre):
    return pre * (lax.erf(pre * (2.0 ** -0.5)) + 1.0) * 0.5


def norm_rows(width, x_s, a_s, m_s, ga, ba, gm, bm):
    tall, wide = 64, 512
    span = width // wide

    def lanes(j):
        return pl.ds(pl.multiple_of(j * wide, wide), wide)

    def fold(v):
        return sum(v[:, k:k + 128] for k in range(0, wide, 128))

    def chunk(i, carry):
        at = pl.ds(pl.multiple_of(i * tall, tall), tall)
        zero = jnp.zeros((tall, 128), F32)
        tot = lax.fori_loop(0, span, lambda j, acc: acc + fold(x_s[at, lanes(j)].astype(F32)), zero)
        mean = jnp.sum(tot, axis=-1, keepdims=True) * (1.0 / width)

        def square(j, acc):
            c = x_s[at, lanes(j)].astype(F32) - mean
            return acc + fold(c * c)

        var = jnp.sum(lax.fori_loop(0, span, square, zero), axis=-1, keepdims=True) * (1.0 / width)
        inv = lax.rsqrt(var + 1e-5)

        def write(j, acc):
            z = (x_s[at, lanes(j)].astype(F32) - mean) * inv
            a_s[at, lanes(j)] = (z * ga[:, lanes(j)] + ba[:, lanes(j)]).astype(BF16)
            m_s[at, lanes(j)] = (z * gm[:, lanes(j)] + bm[:, lanes(j)]).astype(BF16)
            return acc

        return lax.fori_loop(0, span, write, carry)

    lax.fori_loop(0, x_s.shape[0] // tall, chunk, 0)


def front_kernel(nq, nu, x_hbm, wq_ref, wu_ref, ga, ba, gm, bm, qkv_ref, act_ref, xr, x_s, a_s, m_s, pre_s, load_sem, send_sem, recv_sem):
    r, t = pl.program_id(0), pl.program_id(1)
    nt = nq + nu
    even = lax.rem(r, 2) == 0
    is_q = jnp.logical_or(jnp.logical_and(even, t < nq), jnp.logical_and(jnp.logical_not(even), t >= nu))
    mate, cross = peers()
    rows, width = x_s.shape

    def remote(k):
        src = x_hbm if k < 2 else xr.at[1]
        dev = cross if k == 1 else mate
        return pltpu.make_async_remote_copy(src_ref=src, dst_ref=xr.at[k], send_sem=send_sem.at[k], recv_sem=recv_sem.at[k], device_id={'tp': dev}, device_id_type=pl.DeviceIdType.MESH)

    def load(k):
        return pltpu.make_async_copy(x_hbm if k < 0 else xr.at[k], x_s, load_sem)

    @pl.when(jnp.logical_and(r == 0, t == 0))
    def _():
        load(-1).start()
        entry_barrier(mate, cross)
        remote(1).start()
        remote(0).start()

    @pl.when(t == 0)
    def _():
        load(-1).wait()

        norm_rows(width, x_s, a_s, m_s, ga, ba, gm, bm)

    @pl.when(is_q)
    def _():
        qkv_ref[...] = lax.dot_general(wq_ref[...], a_s[...], (((1,), (1,)), ((), ())), preferred_element_type=F32).astype(BF16)

    @pl.when(jnp.logical_not(is_q))
    def _():
        cols = wu_ref.shape[1]
        for c in range(0, cols, 256):
            at = slice(c, c + 256)
            act_ref[:, at] = gelu(pre_s[:, at]).astype(BF16)
            pre_s[:, at] = jnp.dot(m_s[...], wu_ref[:, at], preferred_element_type=F32)

    for k in range(3):
        @pl.when(jnp.logical_and(r == k, t == nt - 2))
        def _():
            remote(k).wait_recv()
            load(k).start()
            if k == 1:
                remote(2).start()

    @pl.when(jnp.logical_and(r == 3, t == nt - 1))
    def _():
        act_ref[...] = gelu(pre_s[...]).astype(BF16)
        for k in range(3):
            remote(k).wait_send()


def front(x, wq, wu, ga, ba, gm, bm):
    rows, width = x.shape
    qcols, ff = wq.shape[0], wu.shape[1]
    tq, tu = 512, 512
    nq, nu = qcols // tq, ff // tu
    nt = nq + nu

    def even(r):
        return lax.rem(r, 2) == 0

    def wq_at(r, t):
        return jnp.where(even(r), jnp.minimum(t, nq - 1), jnp.minimum(nq - 1, nt - 1 - t)), 0

    def wu_at(r, t):
        return 0, jnp.where(even(r), jnp.maximum(t - nq, 0), jnp.maximum(nu - 1 - t, 0))

    def qkv_at(r, t):
        held = jnp.logical_and(jnp.logical_not(even(r)), t < nu)
        return wq_at(r, t)[0], jnp.where(held, r - 1, r)

    def act_at(r, t):
        done = jnp.where(even(r), r * nu + jnp.maximum(t - nq + 1, 0), r * nu + jnp.minimum(t + 1, nu))
        idx = jnp.maximum(done - 2, 0)
        idx = jnp.where(jnp.logical_and(r == 3, t == nt - 1), 4 * nu - 1, idx)
        blk, k = lax.div(idx, nu), lax.rem(idx, nu)
        return blk, jnp.where(even(blk), k, nu - 1 - k)

    vec = pl.BlockSpec((1, width), lambda r, t: (0, 0))
    flops = 2 * 4 * rows * width * (qcols + ff)
    return pl.pallas_call(
        functools.partial(front_kernel, nq, nu),
        grid=(4, nt),
        out_shape=(jax.ShapeDtypeStruct((qcols, 4 * rows), BF16), jax.ShapeDtypeStruct((4 * rows, ff), BF16), jax.ShapeDtypeStruct((3, rows, width), BF16)),
        in_specs=[pl.BlockSpec(memory_space=pl.ANY), pl.BlockSpec((tq, width), wq_at), pl.BlockSpec((width, tu), wu_at), vec, vec, vec, vec],
        out_specs=(pl.BlockSpec((tq, rows), qkv_at), pl.BlockSpec((rows, tu), act_at), pl.BlockSpec(memory_space=pl.ANY)),
        scratch_shapes=[
            pltpu.VMEM((rows, width), BF16),
            pltpu.VMEM((rows, width), BF16),
            pltpu.VMEM((rows, width), BF16),
            pltpu.VMEM((rows, tu), F32),
            pltpu.SemaphoreType.DMA,
            pltpu.SemaphoreType.DMA((3,)),
            pltpu.SemaphoreType.DMA((3,)),
        ],
        compiler_params=pltpu.CompilerParams(collective_id=0, has_side_effects=True, vmem_limit_bytes=VMEM_LIMIT, dimension_semantics=('arbitrary', 'arbitrary')),
        cost_estimate=pl.CostEstimate(flops=flops, bytes_accessed=4 * 2 * width * (qcols + ff), transcendentals=0),
        name='front',
    )(x, wq, wu, ga, ba, gm, bm)[:2]


def attn_kernel(scale, heads_out, tp_ref, qkv_ref, cos_ref, sin_ref, ctx_ref, q_s, k_s, v_s, s_s, p_s, c_s):
    g = pl.program_id(0)
    tp = tp_ref[0]
    half, seq = cos_ref.shape
    hd = 2 * half
    blk = seq // 4
    pad = k_s.shape[1]

    def rel(j):
        return pl.multiple_of((tp ^ j) * blk, blk)

    def rotate(base, j):
        at = pl.ds(rel(j), blk)
        u1 = qkv_ref[base:base + half, at].astype(F32)
        u2 = qkv_ref[base + half:base + hd, at].astype(F32)
        c, s = cos_ref[:, j * blk:(j + 1) * blk], sin_ref[:, j * blk:(j + 1) * blk]
        return jnp.concatenate([u1 * c - u2 * s, u2 * c + u1 * s, jnp.zeros((pad - hd, blk), F32)], axis=0)

    for j in range(4):
        at = slice(j * blk, (j + 1) * blk)
        q_s[:, at] = rotate(0, j).astype(BF16)
        k_s[at, :] = rotate(hd, j).T.astype(BF16)
        v_s[:, at] = qkv_ref[2 * hd:3 * hd, pl.ds(rel(j), blk)]

    base = pl.multiple_of(lax.rem(g, heads_out) * hd, 32)
    for qb in range(4):
        par = qb % 2
        qat = slice(qb * blk, (qb + 1) * blk)
        top = None
        for kb in range(qb + 1):
            kat = slice(kb * blk, (kb + 1) * blk)
            s = jnp.dot(k_s[kat, :], q_s[:, qat], preferred_element_type=F32)
            if kb == qb:
                ki = lax.broadcasted_iota(jnp.int32, (blk, blk), 0)
                qi = lax.broadcasted_iota(jnp.int32, (blk, blk), 1)
                s = jnp.where(ki <= qi, s, -1e30)
            s_s[par, kat, :] = s
            part = jnp.max(s.reshape(blk // 8, 8, blk), axis=0)
            top = part if top is None else jnp.maximum(top, part)
        top = jnp.max(top, axis=0, keepdims=True)
        tot = None
        for kb in range(qb + 1):
            kat = slice(kb * blk, (kb + 1) * blk)
            e = jnp.exp2((s_s[par, kat, :] - top) * (scale * LOG2E))
            s_s[par, kat, :] = e
            part = jnp.sum(e.reshape(blk // 8, 8, blk), axis=0)
            tot = part if tot is None else tot + part
        inv = 1.0 / jnp.sum(tot, axis=0, keepdims=True)
        for kb in range(qb + 1):
            kat = slice(kb * blk, (kb + 1) * blk)
            p_s[par, kat, :] = (s_s[par, kat, :] * inv).astype(BF16)
        nk = (qb + 1) * blk
        ctx = jnp.dot(v_s[:, :nk], p_s[par, :nk, :], preferred_element_type=F32)
        c_s[pl.ds(base, hd), qat] = ctx.astype(BF16)

    @pl.when(lax.rem(g, heads_out) == heads_out - 1)
    def _():
        for j in range(4):
            ctx_ref[pl.ds(rel(j), blk), :] = c_s[:, j * blk:(j + 1) * blk].T


def attention(qkv, cos_tab, sin_tab, tp):
    cols, seq = qkv.shape
    half = cos_tab.shape[0]
    hd = 2 * half
    heads = cols // (3 * hd)
    heads_out = 4
    blk = seq // 4
    tab = pl.BlockSpec((half, seq), lambda g, s: (0, 0))
    return pl.pallas_call(
        functools.partial(attn_kernel, hd ** -0.5, heads_out),
        out_shape=jax.ShapeDtypeStruct((seq, heads * hd), BF16),
        grid_spec=pltpu.PrefetchScalarGridSpec(
            num_scalar_prefetch=1,
            grid=(heads,),
            in_specs=[pl.BlockSpec((3 * hd, seq), lambda g, s: (g, 0)), tab, tab],
            out_specs=pl.BlockSpec((seq, heads_out * hd), lambda g, s: (0, g // heads_out)),
            scratch_shapes=[
                pltpu.VMEM((128, seq), BF16),
                pltpu.VMEM((seq, 128), BF16),
                pltpu.VMEM((hd, seq), BF16),
                pltpu.VMEM((2, seq, blk), F32),
                pltpu.VMEM((2, seq, blk), BF16),
                pltpu.VMEM((heads_out * hd, seq), BF16),
            ],
        ),
        compiler_params=pltpu.CompilerParams(vmem_limit_bytes=VMEM_LIMIT, dimension_semantics=('arbitrary',)),
        cost_estimate=pl.CostEstimate(flops=heads * seq * seq * 2 * 128, bytes_accessed=2 * seq * cols, transcendentals=heads * seq * seq // 2),
        name='attend',
    )(tp, qkv, cos_tab, sin_tab)


def back_kernel(nt, ctx_ref, act_ref, wo_ref, wd_ref, x_ref, out_ref, acc_s, near_s, far_s, recv_s, send_sem, recv_sem):
    p, t = pl.program_id(0), pl.program_id(1)
    tile = jnp.where(lax.rem(p, 2) == 0, t, nt - 1 - t)
    mate, cross = peers()

    def copy(ph, k, src, dev):
        return pltpu.make_async_remote_copy(src_ref=src, dst_ref=recv_s.at[ph, k], send_sem=send_sem.at[ph, k], recv_sem=recv_sem.at[ph, k], device_id={'tp': dev}, device_id_type=pl.DeviceIdType.MESH)

    def near(ph, k):
        return copy(ph, k, near_s.at[lax.rem(k, 3)], mate)

    def far(k):
        return copy(1, k, far_s.at[k], cross)

    @pl.when(jnp.logical_and(p == 0, t == 0))
    def _():
        entry_barrier(mate, cross)

    acc_s[...] = jnp.dot(ctx_ref[...], wo_ref[...], preferred_element_type=F32) + jnp.dot(act_ref[...], wd_ref[...], preferred_element_type=F32)

    @pl.when(p == 0)
    def _():
        @pl.when(t >= 3)
        def _():
            near(0, t - 3).wait_send()

        near_s[lax.rem(t, 3)] = acc_s[...].astype(BF16)
        near(0, t).start()

    @pl.when(p == 1)
    def _():
        near(0, tile).wait_recv()
        far_s[tile] = (acc_s[...] + recv_s[0, tile].astype(F32)).astype(BF16)
        far(tile).start()

    @pl.when(p == 2)
    def _():
        @pl.when(t >= 3)
        def _():
            near(2, t - 3).wait_send()

        @pl.when(t < 3)
        def _():
            near(0, nt - 3 + t).wait_send()

        near_s[lax.rem(t, 3)] = acc_s[...].astype(BF16)
        near(2, t).start()

    @pl.when(p == 3)
    def _():
        near(2, tile).wait_recv()
        far(tile).wait_recv()
        out_ref[...] = (x_ref[...].astype(F32) + acc_s[...] + recv_s[2, tile].astype(F32) + recv_s[1, tile].astype(F32)).astype(BF16)

    @pl.when(jnp.logical_and(p == 3, t == nt - 1))
    def _():
        def drain(k, carry):
            far(k).wait_send()
            return carry

        lax.fori_loop(0, nt, drain, 0)
        for k in range(nt - 3, nt):
            near(2, k).wait_send()


def back(ctx, act, wo, wd, x):
    rows, width = x.shape
    kc, kf = ctx.shape[1], act.shape[1]
    tn = 512
    nt = width // tn

    def tile_at(p, t):
        return 0, jnp.where(lax.rem(p, 2) == 0, t, nt - 1 - t)

    def last_at(p, t):
        return 0, jnp.where(p == 3, nt - 1 - t, nt - 1)

    return pl.pallas_call(
        functools.partial(back_kernel, nt),
        grid=(4, nt),
        out_shape=jax.ShapeDtypeStruct((rows, width), BF16),
        in_specs=[
            pl.BlockSpec((rows, kc), lambda p, t: (3 - p, 0)),
            pl.BlockSpec((rows, kf), lambda p, t: (3 - p, 0)),
            pl.BlockSpec((kc, tn), tile_at),
            pl.BlockSpec((kf, tn), tile_at),
            pl.BlockSpec((rows, tn), last_at),
        ],
        out_specs=pl.BlockSpec((rows, tn), last_at),
        scratch_shapes=[
            pltpu.VMEM((rows, tn), F32),
            pltpu.VMEM((3, rows, tn), BF16),
            pltpu.VMEM((nt, rows, tn), BF16),
            pltpu.VMEM((3, nt, rows, tn), BF16),
            pltpu.SemaphoreType.DMA((3, nt)),
            pltpu.SemaphoreType.DMA((3, nt)),
        ],
        compiler_params=pltpu.CompilerParams(collective_id=1, has_side_effects=True, vmem_limit_bytes=VMEM_LIMIT, dimension_semantics=('arbitrary', 'arbitrary')),
        cost_estimate=pl.CostEstimate(flops=2 * 4 * rows * width * (kc + kf), bytes_accessed=4 * 2 * width * (kc + kf), transcendentals=0),
        name='back',
    )(ctx, act, wo, wd, x)


def solution(mesh):
    def local_layer(hidden_blk, attn_gain, attn_bias, mlp_gain, mlp_bias, w_qkv_part, w_out_part, w_up_part, w_down_part, positions):
        width = hidden_blk.shape[-1]
        x = hidden_blk.reshape(-1, width)
        wq = jnp.transpose(w_qkv_part, (1, 2, 0)).reshape(-1, width)
        half_dim = w_qkv_part.shape[2] // 6
        cos_tab, sin_tab = rotary_tables(positions, half_dim)
        vecs = [v.reshape(1, width) for v in (attn_gain, attn_bias, mlp_gain, mlp_bias)]
        qkv, act = front(x, wq, w_up_part, *vecs)
        tp = lax.axis_index('tp').astype(jnp.int32).reshape(1)
        ctx = attention(qkv, cos_tab, sin_tab, tp)
        out = back(ctx, act, w_out_part, w_down_part, x)
        return out.reshape(hidden_blk.shape)

    return jax.shard_map(local_layer, mesh=mesh, in_specs=(P('dp', 'tp', None), P(), P(), P(), P(), P(None, 'tp', None), P('tp', None), P(None, 'tp'), P('tp', None), P()), out_specs=P('dp', 'tp', None), check_vma=False)
```

time: 1650 us -> 655 us (0.40)
  matrix products: 911 us -> 0 us
  Pallas kernels: 0 us -> 646 us
  waiting for transfers between devices: 481 us -> 0 us
  other arithmetic: 220 us -> 2.36 us
    dot_general x20 -> x0, matrix products: 911 us -> none  [the longest x1 303 us: local_layer(): jnp.einsum('bsf,fd->bsd', up_act, w_down_part, preferred_element_type=jnp...]
    pallas_call x0 -> x3, Pallas kernels: none -> 646 us  [the longest x1 348 us: front(): pl.pallas_call(functools.partial(front_kernel, nq, nu), grid=(4, nt), out...]
    reduce_scatter x1 -> x0, waiting for transfers between devices: 328 us -> none  [local_layer(): lax.psum_scatter(attn_part + mlp_part, 'tp', scatter_dimension=1, tiled=T...]
    all_gather x2 -> x0, waiting for transfers between devices: 152 us -> none  [the longest x1 152 us: local_layer(): attn_in = lax.all_gather(normed_attn, 'tp', axis=1, tiled=True)]
    reduce_sum x10 -> x0, other arithmetic: 136 us -> none  [the longest x8 127 us: one_block(): jnp.sum(exp_scores, axis=-1, keepdims=True)]
    convert_element_type x5 -> x1, other arithmetic: 40.1 us -> 0.01 us  [rotary_tables(): angles = inv_freq[:, None] * positions.astype(F32)[None, :]]
    neg x2 -> x0, other arithmetic: 20.7 us -> none  [apply_rotary(): -vals32[..., half_dim:]]
    squeeze x1 -> x0, other arithmetic: 16.8 us -> none  [attention_branch(): value_seq = qkv_rows[:, :, :, group_size + 1, :]]
  transfers between devices with their start and end apart: 3 -> 0, of which waited for: 2 -> 0; matrix products, arithmetic and copies ran while one was open for 39% -> 0% of each run, Pallas kernels for 0% -> 0%
where the time goes in v1:
time: 655 us
  Pallas kernels  646 us (99%)
    pallas_call x1, Pallas kernels, front(): pl.pallas_call(functools.partial(front_kernel, nq, nu), grid=(4, nt), out...  348 us
    pallas_call x1, Pallas kernels, back(): pl.pallas_call(functools.partial(back_kernel, nt), grid=(4, nt), out_shap...  224 us
    pallas_call x1, Pallas kernels, attention(): pl.pallas_call(functools.partial(attn_kernel, hd ** (-0.5), heads_out), o...  74.5 us

profile of v1, /device:TPU:0, one launch (start us, length us, event | category | flops | bytes accessed | tf_op | source)
XLA Modules:
  0.0 655.1 jit_solution(16852493510386694797)
XLA Ops:
  0.0 0.0 copy-start
  0.0 348.2 %front.1 = (bf16[4608,2048]{1,0:T(8,128)(2,1)}, bf16[2048,6144]{1,0:T(8,128)(2,1)}, bf16[3,512,6144]{2,1,0:T(8,128)(2,1)}) custom-call(bf16[512,6144]{1,0:T(8,128)(2,1)} %bitcast.12, bf16[4608,6144]{1,0:T(8,128)(2,1)} %bitcast.11, bf16[6144,6144]{1,0:T(8,128)(2,1)} %wu_ref.1, f32[1,6144]{1,0:T(1,128)} %bitcast.14, f32[1,6144]{1,0:T(1,128)} %bitcast.15, ...), custom_call_target="tpu_custom_call" | custom-call | flops 270582939648 | bytes 528482304 | tf_op jit(solution)/shard_map/front/pallas_call | solution.py:159
  348.3 0.0 copy-done
  348.3 2.3 multiply_sine_fusion
  350.6 74.5 %attend.1.ctx_ref = bf16[2048,1536]{1,0:T(8,128)(2,1)} custom-call(s32[1]{0:T(128)} %bitcast.tp_ref, bf16[4608,2048]{1,0:T(8,128)(2,1)} %get-tuple-element.7.qkv_ref, f32[48,2048]{1,0:T(8,128)} %get-tuple-element.10.cos_ref, f32[48,2048]{1,0:T(8,128)} %get-tuple-element.9.sin_ref), custom_call_target="tpu_custom_call" | custom-call | flops 17179869184 | bytes 18874368 | tf_op jit(solution)/shard_map/attend/pallas_call | solution.py:249
  425.1 223.8 %back.1 = bf16[512,6144]{1,0:T(8,128)(2,1)} custom-call(bf16[2048,1536]{1,0:T(8,128)(2,1)} %attend.1.ctx_ref, bf16[2048,6144]{1,0:T(8,128)(2,1)} %get-tuple-element.8.act_ref, bf16[1536,6144]{1,0:T(8,128)(2,1)} %wo_ref.1, bf16[6144,6144]{1,0:T(8,128)(2,1)} %wd_ref.1, bf16[512,6144]{1,0:T(8,128)(2,1)} %bitcast.13), custom_call_target="tpu_custom_call" | custom-call | flops 193273528320 | bytes 377487360 | tf_op jit(solution)/shard_map/back/pallas_call | solution.py:349
  648.9 6.2 copy.12
  (2 shorter events, 0.0 us)
Async XLA Ops:
  0.0 348.3 %copy-start = (s32[2048]{0:T(1024)S(1)}, s32[2048]{0:T(1024)}, u32[]{:S(2)}) copy-start(s32[2048]{0:T(1024)} %param.19) | copy-start | bytes 24580

commit v2 on v1

--- a/solution.py
+++ b/solution.py
@@ -37,94 +37,103 @@
     return pre * (lax.erf(pre * (2.0 ** -0.5)) + 1.0) * 0.5
 
 
-def norm_rows(width, x_s, a_s, m_s, ga, ba, gm, bm):
-    tall, wide = 64, 512
-    span = width // wide
-
-    def lanes(j):
-        return pl.ds(pl.multiple_of(j * wide, wide), wide)
+def norm_rows(x_s, a_s, m_s, ga, ba, gm, bm, start, count):
+    tall, wide = 16, 512
+    width = x_s.shape[1]
+    lanes = [slice(j, j + wide) for j in range(0, width, wide)]
 
     def fold(v):
-        return sum(v[:, k:k + 128] for k in range(0, wide, 128))
-
-    def chunk(i, carry):
-        at = pl.ds(pl.multiple_of(i * tall, tall), tall)
-        zero = jnp.zeros((tall, 128), F32)
-        tot = lax.fori_loop(0, span, lambda j, acc: acc + fold(x_s[at, lanes(j)].astype(F32)), zero)
-        mean = jnp.sum(tot, axis=-1, keepdims=True) * (1.0 / width)
-
-        def square(j, acc):
-            c = x_s[at, lanes(j)].astype(F32) - mean
-            return acc + fold(c * c)
-
-        var = jnp.sum(lax.fori_loop(0, span, square, zero), axis=-1, keepdims=True) * (1.0 / width)
-        inv = lax.rsqrt(var + 1e-5)
-
-        def write(j, acc):
-            z = (x_s[at, lanes(j)].astype(F32) - mean) * inv
-            a_s[at, lanes(j)] = (z * ga[:, lanes(j)] + ba[:, lanes(j)]).astype(BF16)
-            m_s[at, lanes(j)] = (z * gm[:, lanes(j)] + bm[:, lanes(j)]).astype(BF16)
-            return acc
-
-        return lax.fori_loop(0, span, write, carry)
-
-    lax.fori_loop(0, x_s.shape[0] // tall, chunk, 0)
-
-
-def front_kernel(nq, nu, x_hbm, wq_ref, wu_ref, ga, ba, gm, bm, qkv_ref, act_ref, xr, x_s, a_s, m_s, pre_s, load_sem, send_sem, recv_sem):
+        return (v[:, 0:128] + v[:, 128:256]) + (v[:, 256:384] + v[:, 384:512])
+
+    for i in range(0, count, tall):
+        at = pl.ds(pl.multiple_of(start + i, tall), tall)
+        mean = jnp.sum(sum(fold(x_s[at, j].astype(F32)) for j in lanes), axis=-1, keepdims=True) * (1.0 / width)
+        tot = 0.0
+        for j in lanes:
+            c = x_s[at, j].astype(F32) - mean
+            tot = tot + fold(c * c)
+        inv = lax.rsqrt(jnp.sum(tot, axis=-1, keepdims=True) * (1.0 / width) + 1e-5)
+        for j in lanes:
+            z = (x_s[at, j].astype(F32) - mean) * inv
+            a_s[0, at, j] = (z * ga[:, j] + ba[:, j]).astype(BF16)
+            m_s[0, at, j] = (z * gm[:, j] + bm[:, j]).astype(BF16)
+
+
+def front_kernel(nq, nu, x_hbm, wq_ref, wu_ref, ga, ba, gm, bm, qkv_ref, act_ref, xr, x_s, a_s, m_s, pre_s, load_sem, send_sem, recv_sem, free_sem):
     r, t = pl.program_id(0), pl.program_id(1)
     nt = nq + nu
-    even = lax.rem(r, 2) == 0
+    here = lax.rem(r, 2)
+    even = here == 0
     is_q = jnp.logical_or(jnp.logical_and(even, t < nq), jnp.logical_and(jnp.logical_not(even), t >= nu))
     mate, cross = peers()
-    rows, width = x_s.shape
 
     def remote(k):
-        src = x_hbm if k < 2 else xr.at[1]
-        dev = cross if k == 1 else mate
-        return pltpu.make_async_remote_copy(src_ref=src, dst_ref=xr.at[k], send_sem=send_sem.at[k], recv_sem=recv_sem.at[k], device_id={'tp': dev}, device_id_type=pl.DeviceIdType.MESH)
-
-    def load(k):
-        return pltpu.make_async_copy(x_hbm if k < 0 else xr.at[k], x_s, load_sem)
+        if k == 0:
+            src, dst, dev = x_hbm, xr, cross
+        else:
+            buf = a_s if k % 2 else m_s
+            src, dst, dev = buf.at[0], buf.at[1], mate
+        return pltpu.make_async_remote_copy(src_ref=src, dst_ref=dst, send_sem=send_sem.at[k], recv_sem=recv_sem.at[k], device_id={'tp': dev}, device_id_type=pl.DeviceIdType.MESH)
+
+    def load(src):
+        return pltpu.make_async_copy(src, x_s, load_sem)
+
+    def norm():
+        load(xr).wait()
+
+        def chunk(i, carry):
+            norm_rows(x_s, a_s, m_s, ga, ba, gm, bm, i * 64, 64)
+            return carry
+
+        lax.fori_loop(0, x_s.shape[0] // 64, chunk, 0)
 
     @pl.when(jnp.logical_and(r == 0, t == 0))
     def _():
-        load(-1).start()
+        load(x_hbm).start()
         entry_barrier(mate, cross)
+        remote(0).start()
+        norm()
         remote(1).start()
-        remote(0).start()
-
-    @pl.when(t == 0)
-    def _():
-        load(-1).wait()
-
-        norm_rows(width, x_s, a_s, m_s, ga, ba, gm, bm)
+        remote(2).start()
+
+    @pl.when(jnp.logical_and(r == 1, t == 0))
+    def _():
+        for k in (1, 2):
+            remote(k).wait()
+
+    @pl.when(jnp.logical_and(r == 1, t == nt - 2))
+    def _():
+        remote(0).wait_recv()
+        load(xr).start()
+
+    @pl.when(jnp.logical_and(r == 2, t == 0))
+    def _():
+        pl.semaphore_signal(free_sem, inc=1, device_id={'tp': mate}, device_id_type=pl.DeviceIdType.MESH)
+        norm()
+        pl.semaphore_wait(free_sem, 1)
+        remote(3).start()
+        remote(4).start()
+
+    @pl.when(jnp.logical_and(r == 3, t == 0))
+    def _():
+        for k in (3, 4):
+            remote(k).wait()
 
     @pl.when(is_q)
     def _():
-        qkv_ref[...] = lax.dot_general(wq_ref[...], a_s[...], (((1,), (1,)), ((), ())), preferred_element_type=F32).astype(BF16)
+        qkv_ref[...] = lax.dot_general(wq_ref[...], a_s[here], (((1,), (1,)), ((), ())), preferred_element_type=F32).astype(BF16)
 
     @pl.when(jnp.logical_not(is_q))
     def _():
-        cols = wu_ref.shape[1]
-        for c in range(0, cols, 256):
+        for c in range(0, wu_ref.shape[1], 256):
             at = slice(c, c + 256)
             act_ref[:, at] = gelu(pre_s[:, at]).astype(BF16)
-            pre_s[:, at] = jnp.dot(m_s[...], wu_ref[:, at], preferred_element_type=F32)
-
-    for k in range(3):
-        @pl.when(jnp.logical_and(r == k, t == nt - 2))
-        def _():
-            remote(k).wait_recv()
-            load(k).start()
-            if k == 1:
-                remote(2).start()
+            pre_s[:, at] = jnp.dot(m_s[here], wu_ref[:, at], preferred_element_type=F32)
 
     @pl.when(jnp.logical_and(r == 3, t == nt - 1))
     def _():
         act_ref[...] = gelu(pre_s[...]).astype(BF16)
-        for k in range(3):
-            remote(k).wait_send()
+        remote(0).wait_send()
 
 
 def front(x, wq, wu, ga, ba, gm, bm):
@@ -148,28 +157,31 @@
         return wq_at(r, t)[0], jnp.where(held, r - 1, r)
 
     def act_at(r, t):
-        done = jnp.where(even(r), r * nu + jnp.maximum(t - nq + 1, 0), r * nu + jnp.minimum(t + 1, nu))
-        idx = jnp.maximum(done - 2, 0)
-        idx = jnp.where(jnp.logical_and(r == 3, t == nt - 1), 4 * nu - 1, idx)
-        blk, k = lax.div(idx, nu), lax.rem(idx, nu)
-        return blk, jnp.where(even(blk), k, nu - 1 - k)
+        k = jnp.where(even(r), t - nq, t)
+        blk = jnp.where(k <= 0, r - 1, r)
+        col = jnp.where(k < 0, nu - 2, jnp.where(k == 0, nu - 1, jnp.minimum(k - 1, nu - 2)))
+        col = jnp.where(jnp.logical_and(r == 3, t == nt - 1), nu - 1, col)
+        col = jnp.where(blk < 0, 0, col)
+        blk = jnp.maximum(blk, 0)
+        return blk, jnp.where(even(blk), col, nu - 1 - col)
 
     vec = pl.BlockSpec((1, width), lambda r, t: (0, 0))
     flops = 2 * 4 * rows * width * (qcols + ff)
     return pl.pallas_call(
         functools.partial(front_kernel, nq, nu),
         grid=(4, nt),
-        out_shape=(jax.ShapeDtypeStruct((qcols, 4 * rows), BF16), jax.ShapeDtypeStruct((4 * rows, ff), BF16), jax.ShapeDtypeStruct((3, rows, width), BF16)),
+        out_shape=(jax.ShapeDtypeStruct((qcols, 4 * rows), BF16), jax.ShapeDtypeStruct((4 * rows, ff), BF16), jax.ShapeDtypeStruct((rows, width), BF16)),
         in_specs=[pl.BlockSpec(memory_space=pl.ANY), pl.BlockSpec((tq, width), wq_at), pl.BlockSpec((width, tu), wu_at), vec, vec, vec, vec],
         out_specs=(pl.BlockSpec((tq, rows), qkv_at), pl.BlockSpec((rows, tu), act_at), pl.BlockSpec(memory_space=pl.ANY)),
         scratch_shapes=[
             pltpu.VMEM((rows, width), BF16),
-            pltpu.VMEM((rows, width), BF16),
-            pltpu.VMEM((rows, width), BF16),
+            pltpu.VMEM((2, rows, width), BF16),
+            pltpu.VMEM((2, rows, width), BF16),
             pltpu.VMEM((rows, tu), F32),
             pltpu.SemaphoreType.DMA,
-            pltpu.SemaphoreType.DMA((3,)),
-            pltpu.SemaphoreType.DMA((3,)),
+            pltpu.SemaphoreType.DMA((5,)),
+            pltpu.SemaphoreType.DMA((5,)),
+            pltpu.SemaphoreType.REGULAR,
         ],
         compiler_params=pltpu.CompilerParams(collective_id=0, has_side_effects=True, vmem_limit_bytes=VMEM_LIMIT, dimension_semantics=('arbitrary', 'arbitrary')),
         cost_estimate=pl.CostEstimate(flops=flops, bytes_accessed=4 * 2 * width * (qcols + ff), transcendentals=0),
@@ -177,13 +189,13 @@
     )(x, wq, wu, ga, ba, gm, bm)[:2]
 
 
-def attn_kernel(scale, heads_out, tp_ref, qkv_ref, cos_ref, sin_ref, ctx_ref, q_s, k_s, v_s, s_s, p_s, c_s):
+def attn_kernel(scale, heads_out, per_step, tp_ref, qkv_ref, cos_ref, sin_ref, ctx_ref, q_s, k_s, v_s, s_s, p_s, c_s):
     g = pl.program_id(0)
     tp = tp_ref[0]
     half, seq = cos_ref.shape
     hd = 2 * half
     blk = seq // 4
-    pad = k_s.shape[1]
+    pad = k_s.shape[2]
 
     def rel(j):
         return pl.multiple_of((tp ^ j) * blk, blk)
@@ -195,44 +207,77 @@
         c, s = cos_ref[:, j * blk:(j + 1) * blk], sin_ref[:, j * blk:(j + 1) * blk]
         return jnp.concatenate([u1 * c - u2 * s, u2 * c + u1 * s, jnp.zeros((pad - hd, blk), F32)], axis=0)
 
-    for j in range(4):
-        at = slice(j * blk, (j + 1) * blk)
-        q_s[:, at] = rotate(0, j).astype(BF16)
-        k_s[at, :] = rotate(hd, j).T.astype(BF16)
-        v_s[:, at] = qkv_ref[2 * hd:3 * hd, pl.ds(rel(j), blk)]
-
-    base = pl.multiple_of(lax.rem(g, heads_out) * hd, 32)
-    for qb in range(4):
-        par = qb % 2
-        qat = slice(qb * blk, (qb + 1) * blk)
-        top = None
-        for kb in range(qb + 1):
-            kat = slice(kb * blk, (kb + 1) * blk)
-            s = jnp.dot(k_s[kat, :], q_s[:, qat], preferred_element_type=F32)
-            if kb == qb:
-                ki = lax.broadcasted_iota(jnp.int32, (blk, blk), 0)
-                qi = lax.broadcasted_iota(jnp.int32, (blk, blk), 1)
-                s = jnp.where(ki <= qi, s, -1e30)
-            s_s[par, kat, :] = s
-            part = jnp.max(s.reshape(blk // 8, 8, blk), axis=0)
-            top = part if top is None else jnp.maximum(top, part)
-        top = jnp.max(top, axis=0, keepdims=True)
-        tot = None
-        for kb in range(qb + 1):
-            kat = slice(kb * blk, (kb + 1) * blk)
-            e = jnp.exp2((s_s[par, kat, :] - top) * (scale * LOG2E))
-            s_s[par, kat, :] = e
-            part = jnp.sum(e.reshape(blk // 8, 8, blk), axis=0)
-            tot = part if tot is None else tot + part
-        inv = 1.0 / jnp.sum(tot, axis=0, keepdims=True)
-        for kb in range(qb + 1):
-            kat = slice(kb * blk, (kb + 1) * blk)
-            p_s[par, kat, :] = (s_s[par, kat, :] * inv).astype(BF16)
+    for h in range(per_step):
+        for j in range(4):
+            at = slice(j * blk, (j + 1) * blk)
+            q_s[h, :, at] = rotate(3 * h * hd, j).astype(BF16)
+            k_s[h, at, :] = rotate((3 * h + 1) * hd, j).T.astype(BF16)
+            v_s[h, :, at] = qkv_ref[(3 * h + 2) * hd:(3 * h + 3) * hd, pl.ds(rel(j), blk)]
+
+    base = pl.multiple_of(lax.rem(g * per_step, heads_out) * hd, 32)
+    tops, sums = {}, {}
+    order = [(0,0),(0,3),(1,0),(1,3),(0,1),(0,2),(1,2),(1,1)]
+
+    def fold(v, op):
+        parts = [v[i:i + 8] for i in range(0, v.shape[0], 8)]
+        while len(parts) > 1:
+            parts = [op(parts[i], parts[i + 1]) for i in range(0, len(parts), 2)]
+        return parts[0]
+
+    def score(u, i):
+        h, qb = order[u]
+        at = slice(i, i + 128)
+        s = jnp.dot(k_s[h, at, :], q_s[h, :, qb * blk:(qb + 1) * blk], preferred_element_type=F32)
+        if i >= qb * blk:
+            ki = i + lax.broadcasted_iota(jnp.int32, (128, blk), 0)
+            qi = qb * blk + lax.broadcasted_iota(jnp.int32, (128, blk), 1)
+            s = jnp.where(ki <= qi, s, -1e30)
+        s_s[u % 3, at, :] = s
+        part = fold(s, jnp.maximum)
+        tops[u] = part if i == 0 else jnp.maximum(tops[u], part)
+
+    def weigh(u, i):
+        if i == 0:
+            tops[u] = jnp.max(tops[u], axis=0, keepdims=True)
+        at = slice(i, i + 32)
+        e = jnp.exp2((s_s[u % 3, at, :] - tops[u]) * (scale * LOG2E))
+        s_s[u % 3, at, :] = e
+        part = fold(e, jnp.add)
+        sums[u] = part if i == 0 else sums[u] + part
+
+    def mix(u, i):
+        if i == 0:
+            sums[u] = 1.0 / jnp.sum(sums[u], axis=0, keepdims=True)
+        at = slice(i, i + 32)
+        p_s[u % 2, at, :] = (s_s[u % 3, at, :] * sums[u]).astype(BF16)
+
+    def finish(u):
+        h, qb = order[u]
         nk = (qb + 1) * blk
-        ctx = jnp.dot(v_s[:, :nk], p_s[par, :nk, :], preferred_element_type=F32)
-        c_s[pl.ds(base, hd), qat] = ctx.astype(BF16)
-
-    @pl.when(lax.rem(g, heads_out) == heads_out - 1)
+        ctx = jnp.dot(v_s[h, :, :nk], p_s[u % 2, :nk, :], preferred_element_type=F32)
+        c_s[pl.ds(base + h * hd, hd), qb * blk:(qb + 1) * blk] = ctx.astype(BF16)
+
+    def stage(fn, u, tall):
+        return [functools.partial(fn, u, i) for i in range(0, (order[u][1] + 1) * blk, tall)]
+
+    def merge(*lists):
+        keyed = [((n + 0.5) / len(each), f) for each in lists for n, f in enumerate(each)]
+        for _, f in sorted(keyed, key=lambda kf: kf[0]):
+            f()
+
+    for n in range(len(order) + 2):
+        lists = []
+        if 0 <= n - 2:
+            lists.append(stage(mix, n - 2, 32))
+        if 0 <= n - 1 < len(order):
+            lists.append(stage(weigh, n - 1, 32))
+        if n < len(order):
+            lists.append(stage(score, n, 128))
+        merge(*lists)
+        if 0 <= n - 2:
+            finish(n - 2)
+
+    @pl.when(lax.rem((g + 1) * per_step, heads_out) == 0)
     def _():
         for j in range(4):
             ctx_ref[pl.ds(rel(j), blk), :] = c_s[:, j * blk:(j + 1) * blk].T
@@ -243,22 +288,22 @@
     half = cos_tab.shape[0]
     hd = 2 * half
     heads = cols // (3 * hd)
-    heads_out = 4
+    heads_out, per_step = 4, 2
     blk = seq // 4
     tab = pl.BlockSpec((half, seq), lambda g, s: (0, 0))
     return pl.pallas_call(
-        functools.partial(attn_kernel, hd ** -0.5, heads_out),
+        functools.partial(attn_kernel, hd ** -0.5, heads_out, per_step),
         out_shape=jax.ShapeDtypeStruct((seq, heads * hd), BF16),
         grid_spec=pltpu.PrefetchScalarGridSpec(
             num_scalar_prefetch=1,
-            grid=(heads,),
-            in_specs=[pl.BlockSpec((3 * hd, seq), lambda g, s: (g, 0)), tab, tab],
-            out_specs=pl.BlockSpec((seq, heads_out * hd), lambda g, s: (0, g // heads_out)),
+            grid=(heads // per_step,),
+            in_specs=[pl.BlockSpec((per_step * 3 * hd, seq), lambda g, s: (g, 0)), tab, tab],
+            out_specs=pl.BlockSpec((seq, heads_out * hd), lambda g, s: (0, g * per_step // heads_out)),
             scratch_shapes=[
-                pltpu.VMEM((128, seq), BF16),
-                pltpu.VMEM((seq, 128), BF16),
-                pltpu.VMEM((hd, seq), BF16),
-                pltpu.VMEM((2, seq, blk), F32),
+                pltpu.VMEM((per_step, 128, seq), BF16),
+                pltpu.VMEM((per_step, seq, 128), BF16),
+                pltpu.VMEM((per_step, hd, seq), BF16),
+                pltpu.VMEM((3, seq, blk), F32),
                 pltpu.VMEM((2, seq, blk), BF16),
                 pltpu.VMEM((heads_out * hd, seq), BF16),
             ],

time: 655 us -> 615 us (0.939)
  Pallas kernels: 646 us -> 606 us
    pallas_call x1, Pallas kernels: 348 us -> 323 us  [front(): pl.pallas_call(functools.partial(front_kernel, nq, nu), grid=(4, nt), out...]
    pallas_call x1, Pallas kernels: 74.5 us -> 59.1 us  [attention(): pl.pallas_call(functools.partial(attn_kernel, hd ** (-0.5), heads_out, pe...]
where the time goes in v2:
time: 615 us
  Pallas kernels  606 us (99%)
  local copies, waits for them, and re-layouts  6.23 us (1%)
    pallas_call x1, Pallas kernels, front(): pl.pallas_call(functools.partial(front_kernel, nq, nu), grid=(4, nt), out...  323 us
    pallas_call x1, Pallas kernels, back(): pl.pallas_call(functools.partial(back_kernel, nt), grid=(4, nt), out_shap...  224 us
    pallas_call x1, Pallas kernels, attention(): pl.pallas_call(functools.partial(attn_kernel, hd ** (-0.5), heads_out, pe...  59.1 us

profile of v2, /device:TPU:0, one launch (start us, length us, event | category | flops | bytes accessed | tf_op | source)
XLA Modules:
  0.0 615.2 jit_solution(11881568353215384271)
XLA Ops:
  0.0 0.7 convert_element_type.3
  0.7 2.3 multiply_sine_fusion
  3.0 323.0 %front.1 = (bf16[4608,2048]{1,0:T(8,128)(2,1)}, bf16[2048,6144]{1,0:T(8,128)(2,1)}, bf16[512,6144]{1,0:T(8,128)(2,1)}) custom-call(bf16[512,6144]{1,0:T(8,128)(2,1)} %bitcast.12, bf16[4608,6144]{1,0:T(8,128)(2,1)} %bitcast.11, bf16[6144,6144]{1,0:T(8,128)(2,1)} %wu_ref.1, f32[1,6144]{1,0:T(1,128)} %bitcast.14, f32[1,6144]{1,0:T(1,128)} %bitcast.15, ...), custom_call_target="tpu_custom_call" | custom-call | flops 270582939648 | bytes 528482304 | tf_op jit(solution)/shard_map/front/pallas_call | solution.py:170
  326.0 59.1 %attend.1.ctx_ref = bf16[2048,1536]{1,0:T(8,128)(2,1)} custom-call(s32[1]{0:T(128)} %bitcast.tp_ref, bf16[4608,2048]{1,0:T(8,128)(2,1)} %get-tuple-element.7.qkv_ref, f32[48,2048]{1,0:T(8,128)} %get-tuple-element.10.cos_ref, f32[48,2048]{1,0:T(8,128)} %get-tuple-element.9.sin_ref), custom_call_target="tpu_custom_call" | custom-call | flops 17179869184 | bytes 18874368 | tf_op jit(solution)/shard_map/attend/pallas_call | solution.py:294
  385.1 223.8 %back.1 = bf16[512,6144]{1,0:T(8,128)(2,1)} custom-call(bf16[2048,1536]{1,0:T(8,128)(2,1)} %attend.1.ctx_ref, bf16[2048,6144]{1,0:T(8,128)(2,1)} %get-tuple-element.8.act_ref, bf16[1536,6144]{1,0:T(8,128)(2,1)} %wo_ref.1, bf16[6144,6144]{1,0:T(8,128)(2,1)} %wd_ref.1, bf16[512,6144]{1,0:T(8,128)(2,1)} %bitcast.13), custom_call_target="tpu_custom_call" | custom-call | flops 193273528320 | bytes 377487360 | tf_op jit(solution)/shard_map/back/pallas_call | solution.py:394
  608.9 6.2 %copy.12 = bf16[1,512,6144]{2,1,0:T(8,128)(2,1)} copy(bf16[1,512,6144]{2,1,0:T(8,128)(2,1)} %bitcast.10) | data formatting | bytes 12582912
  (1 shorter events, 0.0 us)

commit v3 on v2

--- a/solution.py
+++ b/solution.py
@@ -10,6 +10,7 @@
 F32 = jnp.float32
 BF16 = jnp.bfloat16
 VMEM_LIMIT = 67_000_000
+TALL = 64
 LOG2E = 1.4426950408889634
 
 
@@ -37,7 +38,7 @@
     return pre * (lax.erf(pre * (2.0 ** -0.5)) + 1.0) * 0.5
 
 
-def norm_rows(x_s, a_s, m_s, ga, ba, gm, bm, start, count):
+def norm_rows(x_s, a_s, m_s, ga, ba, gm, bm, start):
     tall, wide = 16, 512
     width = x_s.shape[1]
     lanes = [slice(j, j + wide) for j in range(0, width, wide)]
@@ -45,21 +46,22 @@
     def fold(v):
         return (v[:, 0:128] + v[:, 128:256]) + (v[:, 256:384] + v[:, 384:512])
 
-    for i in range(0, count, tall):
+    for i in range(0, TALL, tall):
         at = pl.ds(pl.multiple_of(start + i, tall), tall)
-        mean = jnp.sum(sum(fold(x_s[at, j].astype(F32)) for j in lanes), axis=-1, keepdims=True) * (1.0 / width)
+        src = slice(i, i + tall)
+        mean = jnp.sum(sum(fold(x_s[src, j].astype(F32)) for j in lanes), axis=-1, keepdims=True) * (1.0 / width)
         tot = 0.0
         for j in lanes:
-            c = x_s[at, j].astype(F32) - mean
+            c = x_s[src, j].astype(F32) - mean
             tot = tot + fold(c * c)
         inv = lax.rsqrt(jnp.sum(tot, axis=-1, keepdims=True) * (1.0 / width) + 1e-5)
         for j in lanes:
-            z = (x_s[at, j].astype(F32) - mean) * inv
+            z = (x_s[src, j].astype(F32) - mean) * inv
             a_s[0, at, j] = (z * ga[:, j] + ba[:, j]).astype(BF16)
             m_s[0, at, j] = (z * gm[:, j] + bm[:, j]).astype(BF16)
 
 
-def front_kernel(nq, nu, x_hbm, wq_ref, wu_ref, ga, ba, gm, bm, qkv_ref, act_ref, xr, x_s, a_s, m_s, pre_s, load_sem, send_sem, recv_sem, free_sem):
+def front_kernel(nq, nu, x_hbm, wq_ref, wu_ref, ga_h, ba_h, gm_h, bm_h, qkv_ref, act_ref, xr, x_s, a_s, m_s, pre_s, ga, ba, gm, bm, load_sem, vec_sem, send_sem, recv_sem, free_sem):
     r, t = pl.program_id(0), pl.program_id(1)
     nt = nq + nu
     here = lax.rem(r, 2)
@@ -75,24 +77,36 @@
             src, dst, dev = buf.at[0], buf.at[1], mate
         return pltpu.make_async_remote_copy(src_ref=src, dst_ref=dst, send_sem=send_sem.at[k], recv_sem=recv_sem.at[k], device_id={'tp': dev}, device_id_type=pl.DeviceIdType.MESH)
 
-    def load(src):
-        return pltpu.make_async_copy(src, x_s, load_sem)
-
-    def norm():
-        load(xr).wait()
+    def norm(src):
+        pieces = m_s.shape[1] // TALL
+
+        def load(i):
+            k = lax.rem(i, 2)
+            return pltpu.make_async_copy(src.at[pl.ds(pl.multiple_of(i * TALL, TALL), TALL), :], x_s.at[k], load_sem.at[k])
+
+        load(0).start()
 
         def chunk(i, carry):
-            norm_rows(x_s, a_s, m_s, ga, ba, gm, bm, i * 64, 64)
+            @pl.when(i + 1 < pieces)
+            def _():
+                load(i + 1).start()
+
+            load(i).wait()
+            norm_rows(x_s.at[lax.rem(i, 2)], a_s, m_s, ga, ba, gm, bm, i * TALL)
             return carry
 
-        lax.fori_loop(0, x_s.shape[0] // 64, chunk, 0)
+        lax.fori_loop(0, pieces, chunk, 0)
 
     @pl.when(jnp.logical_and(r == 0, t == 0))
     def _():
-        load(x_hbm).start()
+        vecs = [pltpu.make_async_copy(src, dst, vec_sem.at[k]) for k, (src, dst) in enumerate(((ga_h, ga), (ba_h, ba), (gm_h, gm), (bm_h, bm)))]
+        for each in vecs:
+            each.start()
         entry_barrier(mate, cross)
         remote(0).start()
-        norm()
+        for each in vecs:
+            each.wait()
+        norm(x_hbm)
         remote(1).start()
         remote(2).start()
 
@@ -101,15 +115,11 @@
         for k in (1, 2):
             remote(k).wait()
 
-    @pl.when(jnp.logical_and(r == 1, t == nt - 2))
-    def _():
+    @pl.when(jnp.logical_and(r == 2, t == 0))
+    def _():
+        pl.semaphore_signal(free_sem, inc=1, device_id={'tp': mate}, device_id_type=pl.DeviceIdType.MESH)
         remote(0).wait_recv()
-        load(xr).start()
-
-    @pl.when(jnp.logical_and(r == 2, t == 0))
-    def _():
-        pl.semaphore_signal(free_sem, inc=1, device_id={'tp': mate}, device_id_type=pl.DeviceIdType.MESH)
-        norm()
+        norm(xr)
         pl.semaphore_wait(free_sem, 1)
         remote(3).start()
         remote(4).start()
@@ -121,7 +131,9 @@
 
     @pl.when(is_q)
     def _():
-        qkv_ref[...] = lax.dot_general(wq_ref[...], a_s[here], (((1,), (1,)), ((), ())), preferred_element_type=F32).astype(BF16)
+        for c in range(0, wq_ref.shape[0], 256):
+            at = slice(c, c + 256)
+            qkv_ref[at, :] = lax.dot_general(wq_ref[at, :], a_s[here], (((1,), (1,)), ((), ())), preferred_element_type=F32).astype(BF16)
 
     @pl.when(jnp.logical_not(is_q))
     def _():
@@ -132,14 +144,16 @@
 
     @pl.when(jnp.logical_and(r == 3, t == nt - 1))
     def _():
-        act_ref[...] = gelu(pre_s[...]).astype(BF16)
+        for c in range(0, wu_ref.shape[1], 256):
+            at = slice(c, c + 256)
+            act_ref[:, at] = gelu(pre_s[:, at]).astype(BF16)
         remote(0).wait_send()
 
 
 def front(x, wq, wu, ga, ba, gm, bm):
     rows, width = x.shape
     qcols, ff = wq.shape[0], wu.shape[1]
-    tq, tu = 512, 512
+    tq, tu = 512, 768
     nq, nu = qcols // tq, ff // tu
     nt = nq + nu
 
@@ -165,20 +179,24 @@
         blk = jnp.maximum(blk, 0)
         return blk, jnp.where(even(blk), col, nu - 1 - col)
 
-    vec = pl.BlockSpec((1, width), lambda r, t: (0, 0))
     flops = 2 * 4 * rows * width * (qcols + ff)
     return pl.pallas_call(
         functools.partial(front_kernel, nq, nu),
         grid=(4, nt),
         out_shape=(jax.ShapeDtypeStruct((qcols, 4 * rows), BF16), jax.ShapeDtypeStruct((4 * rows, ff), BF16), jax.ShapeDtypeStruct((rows, width), BF16)),
-        in_specs=[pl.BlockSpec(memory_space=pl.ANY), pl.BlockSpec((tq, width), wq_at), pl.BlockSpec((width, tu), wu_at), vec, vec, vec, vec],
+        in_specs=[pl.BlockSpec(memory_space=pl.ANY), pl.BlockSpec((tq, width), wq_at), pl.BlockSpec((width, tu), wu_at)] + [pl.BlockSpec(memory_space=pl.ANY)] * 4,
         out_specs=(pl.BlockSpec((tq, rows), qkv_at), pl.BlockSpec((rows, tu), act_at), pl.BlockSpec(memory_space=pl.ANY)),
         scratch_shapes=[
-            pltpu.VMEM((rows, width), BF16),
+            pltpu.VMEM((2, TALL, width), BF16),
             pltpu.VMEM((2, rows, width), BF16),
             pltpu.VMEM((2, rows, width), BF16),
             pltpu.VMEM((rows, tu), F32),
-            pltpu.SemaphoreType.DMA,
+            pltpu.VMEM((1, width), F32),
+            pltpu.VMEM((1, width), F32),
+            pltpu.VMEM((1, width), F32),
+            pltpu.VMEM((1, width), F32),
+            pltpu.SemaphoreType.DMA((2,)),
+            pltpu.SemaphoreType.DMA((4,)),
             pltpu.SemaphoreType.DMA((5,)),
             pltpu.SemaphoreType.DMA((5,)),
             pltpu.SemaphoreType.REGULAR,
@@ -314,7 +332,7 @@
     )(tp, qkv, cos_tab, sin_tab)
 
 
-def back_kernel(nt, ctx_ref, act_ref, wo_ref, wd_ref, x_ref, out_ref, acc_s, near_s, far_s, recv_s, send_sem, recv_sem):
+def back_kernel(nt, ctx_ref, act_ref, wo_ref, wd_ref, x_ref, out_ref, acc_s, near_s, recv_s, send_sem, recv_sem):
     p, t = pl.program_id(0), pl.program_id(1)
     tile = jnp.where(lax.rem(p, 2) == 0, t, nt - 1 - t)
     mate, cross = peers()
@@ -322,17 +340,26 @@
     def copy(ph, k, src, dev):
         return pltpu.make_async_remote_copy(src_ref=src, dst_ref=recv_s.at[ph, k], send_sem=send_sem.at[ph, k], recv_sem=recv_sem.at[ph, k], device_id={'tp': dev}, device_id_type=pl.DeviceIdType.MESH)
 
+    def by_rows(add):
+        def chunk(i, carry):
+            add(pl.ds(pl.multiple_of(i * 64, 64), 64))
+            return carry
+
+        lax.fori_loop(0, acc_s.shape[0] // 64, chunk, 0)
+
     def near(ph, k):
         return copy(ph, k, near_s.at[lax.rem(k, 3)], mate)
 
     def far(k):
-        return copy(1, k, far_s.at[k], cross)
+        return copy(1, k, recv_s.at[0, k], cross)
 
     @pl.when(jnp.logical_and(p == 0, t == 0))
     def _():
         entry_barrier(mate, cross)
 
-    acc_s[...] = jnp.dot(ctx_ref[...], wo_ref[...], preferred_element_type=F32) + jnp.dot(act_ref[...], wd_ref[...], preferred_element_type=F32)
+    for c in range(0, acc_s.shape[1], 256):
+        at = slice(c, c + 256)
+        acc_s[:, at] = jnp.dot(ctx_ref[...], wo_ref[:, at], preferred_element_type=F32) + jnp.dot(act_ref[...], wd_ref[:, at], preferred_element_type=F32)
 
     @pl.when(p == 0)
     def _():
@@ -346,7 +373,11 @@
     @pl.when(p == 1)
     def _():
         near(0, tile).wait_recv()
-        far_s[tile] = (acc_s[...] + recv_s[0, tile].astype(F32)).astype(BF16)
+
+        def add(at):
+            recv_s[0, tile, at, :] = (acc_s[at, :] + recv_s[0, tile, at, :].astype(F32)).astype(BF16)
+
+        by_rows(add)
         far(tile).start()
 
     @pl.when(p == 2)
@@ -355,9 +386,10 @@
         def _():
             near(2, t - 3).wait_send()
 
-        @pl.when(t < 3)
+        @pl.when(t == 0)
         def _():
-            near(0, nt - 3 + t).wait_send()
+            for k in range(nt - 3, nt):
+                near(0, k).wait_send()
 
         near_s[lax.rem(t, 3)] = acc_s[...].astype(BF16)
         near(2, t).start()
@@ -366,7 +398,11 @@
     def _():
         near(2, tile).wait_recv()
         far(tile).wait_recv()
-        out_ref[...] = (x_ref[...].astype(F32) + acc_s[...] + recv_s[2, tile].astype(F32) + recv_s[1, tile].astype(F32)).astype(BF16)
+
+        def add(at):
+            out_ref[at, :] = (x_ref[at, :].astype(F32) + acc_s[at, :] + recv_s[2, tile, at, :].astype(F32) + recv_s[1, tile, at, :].astype(F32)).astype(BF16)
+
+        by_rows(add)
 
     @pl.when(jnp.logical_and(p == 3, t == nt - 1))
     def _():
@@ -382,7 +418,7 @@
 def back(ctx, act, wo, wd, x):
     rows, width = x.shape
     kc, kf = ctx.shape[1], act.shape[1]
-    tn = 512
+    tn = 768
     nt = width // tn
 
     def tile_at(p, t):
@@ -406,7 +442,6 @@
         scratch_shapes=[
             pltpu.VMEM((rows, tn), F32),
             pltpu.VMEM((3, rows, tn), BF16),
-            pltpu.VMEM((nt, rows, tn), BF16),
             pltpu.VMEM((3, nt, rows, tn), BF16),
             pltpu.SemaphoreType.DMA((3, nt)),
             pltpu.SemaphoreType.DMA((3, nt)),

time: 615 us -> 613 us (level)
  no operation moved by 1% of the time
where the time goes in v3:
time: 613 us; the launch traced here: 612 us
  Pallas kernels  603 us (98%)
  local copies, waits for them, and re-layouts  6.23 us (1%)
    pallas_call x1, Pallas kernels, front(): pl.pallas_call(functools.partial(front_kernel, nq, nu), grid=(4, nt), out...  324 us
    pallas_call x1, Pallas kernels, back(): pl.pallas_call(functools.partial(back_kernel, nt), grid=(4, nt), out_shap...  220 us
    pallas_call x1, Pallas kernels, attention(): pl.pallas_call(functools.partial(attn_kernel, hd ** (-0.5), heads_out, pe...  59.1 us

profile of v3, /device:TPU:0, one launch (start us, length us, event | category | flops | bytes accessed | tf_op | source)
XLA Modules:
  0.0 612.3 jit_solution(11282717626856713186)
XLA Ops:
  0.0 0.7 convert_element_type.3
  0.7 2.3 multiply_sine_fusion
  3.0 324.4 %front.1 = (bf16[4608,2048]{1,0:T(8,128)(2,1)}, bf16[2048,6144]{1,0:T(8,128)(2,1)}, bf16[512,6144]{1,0:T(8,128)(2,1)}) custom-call(bf16[512,6144]{1,0:T(8,128)(2,1)} %bitcast.12, bf16[4608,6144]{1,0:T(8,128)(2,1)} %bitcast.11, bf16[6144,6144]{1,0:T(8,128)(2,1)} %wu_ref.1, f32[1,6144]{1,0:T(1,128)} %bitcast.14, f32[1,6144]{1,0:T(1,128)} %bitcast.15, ...), custom_call_target="tpu_custom_call" | custom-call | flops 270582939648 | bytes 528482304 | tf_op jit(solution)/shard_map/front/pallas_call | solution.py:183
  327.4 59.1 %attend.1.ctx_ref = bf16[2048,1536]{1,0:T(8,128)(2,1)} custom-call(s32[1]{0:T(128)} %bitcast.tp_ref, bf16[4608,2048]{1,0:T(8,128)(2,1)} %get-tuple-element.7.qkv_ref, f32[48,2048]{1,0:T(8,128)} %get-tuple-element.10.cos_ref, f32[48,2048]{1,0:T(8,128)} %get-tuple-element.9.sin_ref), custom_call_target="tpu_custom_call" | custom-call | flops 17179869184 | bytes 18874368 | tf_op jit(solution)/shard_map/attend/pallas_call | solution.py:312
  386.5 219.6 %back.1 = bf16[512,6144]{1,0:T(8,128)(2,1)} custom-call(bf16[2048,1536]{1,0:T(8,128)(2,1)} %attend.1.ctx_ref, bf16[2048,6144]{1,0:T(8,128)(2,1)} %get-tuple-element.8.act_ref, bf16[1536,6144]{1,0:T(8,128)(2,1)} %wo_ref.1, bf16[6144,6144]{1,0:T(8,128)(2,1)} %wd_ref.1, bf16[512,6144]{1,0:T(8,128)(2,1)} %bitcast.13), custom_call_target="tpu_custom_call" | custom-call | flops 193273528320 | bytes 377487360 | tf_op jit(solution)/shard_map/back/pallas_call | solution.py:430
  606.0 6.2 %copy.12 = bf16[1,512,6144]{2,1,0:T(8,128)(2,1)} copy(bf16[1,512,6144]{2,1,0:T(8,128)(2,1)} %bitcast.10) | data formatting | bytes 12582912
  (1 shorter events, 0.0 us)

commit v4 on v3

--- a/solution.py
+++ b/solution.py
@@ -345,7 +345,7 @@
             add(pl.ds(pl.multiple_of(i * 64, 64), 64))
             return carry
 
-        lax.fori_loop(0, acc_s.shape[0] // 64, chunk, 0)
+        lax.fori_loop(0, acc_s.shape[0] // 64, chunk, 0, unroll=2)
 
     def near(ph, k):
         return copy(ph, k, near_s.at[lax.rem(k, 3)], mate)
@@ -452,6 +452,26 @@
     )(ctx, act, wo, wd, x)
 
 
+def copy_kernel(src_ref, dst_ref):
+    dst_ref[...] = src_ref[...]
+
+
+def hand_over(y):
+    rows, width = y.shape
+    tall = rows // 8
+    spec = pl.BlockSpec((tall, width), lambda i: (i, 0))
+    return pl.pallas_call(
+        copy_kernel,
+        grid=(8,),
+        out_shape=jax.ShapeDtypeStruct(y.shape, y.dtype),
+        in_specs=[spec],
+        out_specs=spec,
+        compiler_params=pltpu.CompilerParams(dimension_semantics=('arbitrary',)),
+        cost_estimate=pl.CostEstimate(flops=0, bytes_accessed=4 * rows * width, transcendentals=0),
+        name='hand_over',
+    )(y)
+
+
 def solution(mesh):
     def local_layer(hidden_blk, attn_gain, attn_bias, mlp_gain, mlp_bias, w_qkv_part, w_out_part, w_up_part, w_down_part, positions):
         width = hidden_blk.shape[-1]
@@ -464,6 +484,6 @@
         tp = lax.axis_index('tp').astype(jnp.int32).reshape(1)
         ctx = attention(qkv, cos_tab, sin_tab, tp)
         out = back(ctx, act, w_out_part, w_down_part, x)
-        return out.reshape(hidden_blk.shape)
+        return hand_over(out).reshape(hidden_blk.shape)
 
     return jax.shard_map(local_layer, mesh=mesh, in_specs=(P('dp', 'tp', None), P(), P(), P(), P(), P(None, 'tp', None), P('tp', None), P(None, 'tp'), P('tp', None), P()), out_specs=P('dp', 'tp', None), check_vma=False)

time: 613 us -> 615 us (level)
  Pallas kernels: 603 us -> 611 us
  local copies, waits for them, and re-layouts: 6.23 us -> 0 us
    pallas_call x0 -> x1, Pallas kernels: none -> 7.82 us  [hand_over(): pl.pallas_call(copy_kernel, grid=(8,), out_shape=jax.ShapeDtypeStruct(y.s...]
    unnamed x1 -> x0, local copies, waits for them, and re-layouts: 6.23 us -> none
where the time goes in v4:
time: 615 us; the launch traced here: 614 us
  Pallas kernels  611 us (99%)
    pallas_call x1, Pallas kernels, front(): pl.pallas_call(functools.partial(front_kernel, nq, nu), grid=(4, nt), out...  324 us
    pallas_call x1, Pallas kernels, back(): pl.pallas_call(functools.partial(back_kernel, nt), grid=(4, nt), out_shap...  220 us
    pallas_call x1, Pallas kernels, attention(): pl.pallas_call(functools.partial(attn_kernel, hd ** (-0.5), heads_out, pe...  59.1 us

profile of v4, /device:TPU:0, one launch (start us, length us, event | category | flops | bytes accessed | tf_op | source)
XLA Modules:
  0.0 614.3 jit_solution(15939015897088117012)
XLA Ops:
  0.0 0.7 convert_element_type.3
  0.7 2.3 multiply_sine_fusion
  3.0 324.4 %front.1 = (bf16[4608,2048]{1,0:T(8,128)(2,1)}, bf16[2048,6144]{1,0:T(8,128)(2,1)}, bf16[512,6144]{1,0:T(8,128)(2,1)}) custom-call(bf16[512,6144]{1,0:T(8,128)(2,1)} %bitcast.11, bf16[4608,6144]{1,0:T(8,128)(2,1)} %bitcast.10, bf16[6144,6144]{1,0:T(8,128)(2,1)} %wu_ref.1, f32[1,6144]{1,0:T(1,128)} %bitcast.13, f32[1,6144]{1,0:T(1,128)} %bitcast.14, ...), custom_call_target="tpu_custom_call" | custom-call | flops 270582939648 | bytes 528482304 | tf_op jit(solution)/shard_map/front/pallas_call | solution.py:183
  327.4 59.1 %attend.1.ctx_ref = bf16[2048,1536]{1,0:T(8,128)(2,1)} custom-call(s32[1]{0:T(128)} %bitcast.tp_ref, bf16[4608,2048]{1,0:T(8,128)(2,1)} %get-tuple-element.7.qkv_ref, f32[48,2048]{1,0:T(8,128)} %get-tuple-element.10.cos_ref, f32[48,2048]{1,0:T(8,128)} %get-tuple-element.9.sin_ref), custom_call_target="tpu_custom_call" | custom-call | flops 17179869184 | bytes 18874368 | tf_op jit(solution)/shard_map/attend/pallas_call | solution.py:312
  386.5 220.0 %back.1.src_ref = bf16[512,6144]{1,0:T(8,128)(2,1)} custom-call(bf16[2048,1536]{1,0:T(8,128)(2,1)} %attend.1.ctx_ref, bf16[2048,6144]{1,0:T(8,128)(2,1)} %get-tuple-element.8.act_ref, bf16[1536,6144]{1,0:T(8,128)(2,1)} %wo_ref.1, bf16[6144,6144]{1,0:T(8,128)(2,1)} %wd_ref.1, bf16[512,6144]{1,0:T(8,128)(2,1)} %bitcast.12), custom_call_target="tpu_custom_call" | custom-call | flops 193273528320 | bytes 377487360 | tf_op jit(solution)/shard_map/back/pallas_call | solution.py:430
  606.5 7.8 %hand_over.1 = bf16[512,6144]{1,0:T(8,128)(2,1)} custom-call(bf16[512,6144]{1,0:T(8,128)(2,1)} %back.1.src_ref), custom_call_target="tpu_custom_call" | custom-call | bytes 12582912 | tf_op jit(solution)/shard_map/hand_over/pallas_call | solution.py:463
  (1 shorter events, 0.0 us)
